TPU v7x, 64 devices: a 2x2x8 block of a 4x4x8 slice. The times are simulated.
64 devices in a mesh: data: 4 (over x, y), seq: 16 (over z, core).
Axes of the slice: x: 2, y: 2, z: 8, core: 2. Of those that a mesh axis runs over, the one named last changes fastest.
The devices are a block of a 4x4x8 slice.
Arguments:
- patches: bfloat16 [256, 512, 512], P('data', 'seq'), parts along dimension 0
- ln1_gain: float32 [512], replicated
- ln1_bias: float32 [512], replicated
- w_in: bfloat16 [512, 3072], replicated
- b_in: float32 [3072], replicated
- ln2_gain: float32 [1536], replicated
- ln2_bias: float32 [1536], replicated
- w_spatial: bfloat16 [512, 512], replicated
- b_spatial: float32 [512], replicated
- w_out: bfloat16 [1536, 512], replicated
- b_out: float32 [512], replicated
Outputs:
- output: bfloat16 [256, 512, 512], P('data', 'seq'), parts along dimension 0
There are 4 independent parts. A program takes and returns all parts, laid end to end along the dimension named above; an argument that names none is the same for every part.
All inputs are finite; a program needn't handle non-finite values.
Results may differ from a plain program's by a relative error of at most 0.00927909.
Values are sent between devices in bfloat16 or wider.
A program may use at most 768 MiB of HBM per device.

v0:
```python
import jax
import jax.numpy as jnp
from jax import lax
from jax.sharding import PartitionSpec as P, NamedSharding

LN_EPS = 1e-6


def layer_norm(values, gain_vec, offset):
    values_f = values.astype(jnp.float32)
    mean_val = jnp.mean(values_f, axis=-1, keepdims=True)
    centered = values_f - mean_val
    var_val = jnp.mean(centered * centered, axis=-1, keepdims=True)
    return (centered * lax.rsqrt(var_val + LN_EPS) * gain_vec + offset).astype(jnp.bfloat16)


def gelu_proj(normed, weight, offset):
    hidden = jnp.einsum("bsc,cf->bsf", normed, weight, preferred_element_type=jnp.float32) + offset
    return jax.nn.gelu(hidden, approximate=False).astype(jnp.bfloat16)


def solution(mesh):
    row_spec = P("data", "seq", None)
    vec_spec = P(None)
    mat_spec = P(None, None)
    in_specs = (row_spec, vec_spec, vec_spec, mat_spec, vec_spec, vec_spec, vec_spec, mat_spec, vec_spec, mat_spec, vec_spec)

    def per_device(patches, ln1_gain, ln1_bias, w_in, b_in, ln2_gain, ln2_bias, w_spatial, b_spatial, w_out, b_out):
        half_dim = w_out.shape[0]
        local_rows = patches.shape[1]
        normed = layer_norm(patches, ln1_gain, ln1_bias)
        gate_a = gelu_proj(normed, w_in[:, :half_dim], b_in[:half_dim])
        gate_n = layer_norm(gelu_proj(normed, w_in[:, half_dim:], b_in[half_dim:]), ln2_gain, ln2_bias)
        by_channel = lax.all_to_all(gate_n, "seq", 2, 1, tiled=True)
        spatial = jnp.einsum("rs,bre->bse", w_spatial, by_channel, preferred_element_type=jnp.float32).astype(jnp.bfloat16)
        by_patch = lax.all_to_all(spatial, "seq", 1, 2, tiled=True)
        local_bias = lax.dynamic_slice_in_dim(b_spatial, lax.axis_index("seq") * local_rows, local_rows)
        gated = (gate_a.astype(jnp.float32) * (by_patch.astype(jnp.float32) + local_bias[:, None])).astype(jnp.bfloat16)
        mixed = jnp.einsum("bse,ec->bsc", gated, w_out, preferred_element_type=jnp.float32) + b_out
        return (patches.astype(jnp.float32) + mixed).astype(jnp.bfloat16)

    return jax.shard_map(per_device, mesh=mesh, in_specs=in_specs, out_specs=row_spec, check_vma=False)
```

profile of v0, /device:TPU:21, one launch (start us, length us, event | category | flops | bytes accessed | tf_op | source)
XLA Modules:
  0.0 589.9 jit_solution(3318532496595164188)
XLA Ops:
  0.0 2.1 convert_reduce_fusion.1
  2.1 2.5 fusion.29
  4.6 1.4 fusion.81
  6.0 32.6 %convert_reduce_fusion = (f32[64,32]{1,0:T(8,128)S(1)}, bf16[64,32,1536]{2,1,0:T(8,128)(2,1)S(1)}) fusion(f32[1536]{0:T(1024)S(1)} %get-tuple-element.6, bf16[512,3072]{1,0:T(8,128)(2,1)} %param.14, bf16[64,32,512]{2,1,0:T(8,128)(2,1)} %param.11, f32[512]{0:T(512)} %param.13, f32[512]{0:T(512)} %param.12, f32[64,32]{1,0:T(8,128)S(1)} %add_rsqrt_fusion.1, ...), kind=kOutput, calls=%fused_computation.4 | convolution fusion | flops 3441424384 | bytes 9996288 | tf_op jit(solution)/shard_map/bsc,cf->bsf/dot_general | solution.py:18
  38.7 1.8 fusion.2
  40.5 4.5 fusion.5
  45.0 22.5 %copy.24 = bf16[64,32,1536]{0,1,2:T(8,128)(2,1)} copy(bf16[64,32,1536]{2,1,0:T(8,128)(2,1)} %fusion.5) | data formatting | bytes 12582912 | tf_op jit(solution)/shard_map/convert_element_type | solution.py:14
  67.5 16.6 %reshape.42 = bf16[16,2,98304]{2,1,0:T(2,128)(2,1)} reshape(bf16[1536,32,64]{2,1,0:T(8,128)(2,1)} %bitcast.35) | data formatting | bytes 12582912
  84.1 151.5 %all_to_all.27 = bf16[16,2,98304]{2,1,0:T(2,128)(2,1)} all-to-all(bf16[16,2,98304]{2,1,0:T(2,128)(2,1)} %reshape.42), channel_id=1, replica_groups=mesh['data'=4,'seq'=16] {'seq'}, dimensions={0} | all-to-all | bytes 12582912 | tf_op jit(solution)/shard_map/all_to_all | solution.py:34
  235.6 16.3 %reshape.43 = bf16[1536,32,64]{2,1,0:T(8,128)(2,1)} reshape(bf16[16,2,98304]{2,1,0:T(2,128)(2,1)} %all_to_all.27) | data formatting | bytes 12582912
  251.9 23.1 %copy.25 = bf16[64,32,16,96]{3,1,2,0:T(8,128)(2,1)} copy(bf16[64,32,16,96]{0,1,3,2:T(8,128)(2,1)} %bitcast.36) | data formatting | bytes 12582912 | tf_op jit(solution)/shard_map/all_to_all | solution.py:34
  275.0 10.0 %convert_bitcast_fusion.1 = bf16[64,512,96]{1,2,0:T(8,128)(2,1)} fusion(bf16[64,512,96]{2,1,0:T(8,128)(2,1)} %bitcast.34, bf16[512,512]{1,0:T(8,128)(2,1)S(1)} %copy-done.1), kind=kOutput, calls=%fused_computation.48 | convolution fusion | flops 3224371200 | bytes 13107200 | tf_op jit(solution)/shard_map/rs,bre->bse/dot_general | solution.py:35
  285.0 11.5 %copy.27 = bf16[64,512,96]{2,0,1:T(8,128)(2,1)} copy(bf16[64,512,96]{1,2,0:T(8,128)(2,1)} %convert_bitcast_fusion.1) | data formatting | bytes 12582912 | tf_op jit(solution)/shard_map/convert_element_type | solution.py:35
  296.5 5.3 all-to-all-start.1
  301.9 0.8 dynamic_slice.3
  302.6 188.5 %all-to-all-done.1 = bf16[64,512,96]{2,0,1:T(8,128)(2,1)} async-done(((bf16[64,512,96]{2,0,1:T(8,128)(2,1)}), bf16[64,512,96]{2,0,1:T(8,128)(2,1)}, u32[]{:S(2)}, u32[]{:S(2)}) %all-to-all-start.1) | async-done | bytes 6291488 | tf_op jit(solution)/shard_map/all_to_all | solution.py:36
  491.2 12.0 %copy.28 = bf16[64,512,96]{2,1,0:T(8,128)(2,1)} copy(bf16[64,512,96]{2,0,1:T(8,128)(2,1)} %all-to-all-done.1) | data formatting | bytes 12582912 | tf_op jit(solution)/shard_map/all_to_all | solution.py:36
  503.2 11.5 %convert_bitcast_fusion = f32[64,32,16,96]{3,1,2,0:T(8,128)} fusion(bf16[64,16,32,96]{3,2,1,0:T(8,128)(2,1)} %bitcast.37), kind=kLoop, calls=%fused_computation.2 | loop fusion | flops 3145728 | bytes 18874368 | tf_op jit(solution)/shard_map/convert_element_type | solution.py:38
  514.7 20.1 %copy.29 = f32[64,32,16,96]{3,2,1,0:T(8,128)} copy(f32[64,32,16,96]{3,1,2,0:T(8,128)} %convert_bitcast_fusion) | data formatting | bytes 25165824 | tf_op jit(solution)/shard_map/convert_element_type | solution.py:38
  534.7 18.1 %reshape.36 = f32[64,32,1536]{2,1,0:T(8,128)} reshape(f32[64,32,16,96]{3,2,1,0:T(8,128)} %copy.29) | data formatting | bytes 25165824 | tf_op jit(solution)/shard_map/convert_element_type | solution.py:38
  552.8 0.0 copy-done.5
  552.8 0.0 copy-done.6
  552.9 0.0 copy-done.7
  552.9 36.8 %fusion.33 = bf16[64,32,512]{2,1,0:T(8,128)(2,1)} fusion(bf16[64,32,512]{2,1,0:T(8,128)(2,1)} %param.11, f32[512]{0:T(512)S(1)} %copy-done.5, bf16[1536,512]{1,0:T(8,128)(2,1)S(1)} %copy-done, f32[64,32,1536]{2,1,0:T(8,128)} %reshape.36, f32[32]{0:T(128)S(1)} %dynamic_slice.3, f32[1536]{0:T(1024)S(1)} %copy-done.4, bf16[512,3072]{1,0:T(8,128)(2,1)} %param.14, ...), kind=kOutput, calls=%fused_computation.59 | convolution fusion | flops 6673137664 | bytes 22048896 | tf_op jit(solution)/shard_map/bse,ec->bsc/dot_general | solution.py:39
  (17 shorter events, 0.1 us)
Async XLA Ops:
  0.0 552.8 %copy-start = (bf16[1536,512]{1,0:T(8,128)(2,1)S(1)}, bf16[1536,512]{1,0:T(8,128)(2,1)}, u32[]{:S(2)}) copy-start(bf16[1536,512]{1,0:T(8,128)(2,1)} %param.20) | copy-start | bytes 4718596
  6.0 34.5 %copy-start.2 = (f32[1536]{0:T(1024)S(1)}, f32[1536]{0:T(1024)}, u32[]{:S(2)}) copy-start(f32[1536]{0:T(1024)} %param.17) | copy-start | bytes 18436
  6.0 34.5 %copy-start.3 = (f32[1536]{0:T(1024)S(1)}, f32[1536]{0:T(1024)}, u32[]{:S(2)}) copy-start(f32[1536]{0:T(1024)} %param.16) | copy-start | bytes 18436
  251.9 23.1 %copy-start.1 = (bf16[512,512]{1,0:T(8,128)(2,1)S(1)}, bf16[512,512]{1,0:T(8,128)(2,1)}, u32[]{:S(2)}) copy-start(bf16[512,512]{1,0:T(8,128)(2,1)} %param.18) | copy-start | bytes 1572868
  296.5 194.6 %all-to-all-start.1 = ((bf16[64,512,96]{2,0,1:T(8,128)(2,1)}), bf16[64,512,96]{2,0,1:T(8,128)(2,1)}, u32[]{:S(2)}, u32[]{:S(2)}) async-start(bf16[64,512,96]{2,0,1:T(8,128)(2,1)} %copy.27), calls=%async_computation.1 | async-start | bytes 16777216 | tf_op jit(solution)/shard_map/all_to_all | solution.py:36
  534.7 18.1 %copy-start.4 = (f32[1536]{0:T(1024)S(1)}, f32[1536]{0:T(1024)}, u32[]{:S(2)}) copy-start(f32[1536]{0:T(1024)} %get-tuple-element.5) | copy-start | bytes 18436
  534.7 18.1 %copy-start.5 = (f32[512]{0:T(512)S(1)}, f32[512]{0:T(512)}, u32[]{:S(2)}) copy-start(f32[512]{0:T(512)} %param.21) | copy-start | bytes 6148
  534.7 18.1 %copy-start.6 = (f32[512]{0:T(512)S(1)}, f32[512]{0:T(512)}, u32[]{:S(2)}) copy-start(f32[512]{0:T(512)} %param.13) | copy-start | bytes 6148
  534.7 18.1 %copy-start.7 = (f32[512]{0:T(512)S(1)}, f32[512]{0:T(512)}, u32[]{:S(2)}) copy-start(f32[512]{0:T(512)} %param.12) | copy-start | bytes 6148
where the time goes:
time: 601 us; the launch traced here: 590 us
  waiting for transfers between devices  189 us (31%)
  blocking collectives  151 us (25%)
  local copies, waits for them, and re-layouts  142 us (24%)
  matrix products  79.5 us (13%)
  other arithmetic  22.4 us (4%)
    all_to_all x1, waiting for transfers between devices, per_device(): by_patch = lax.all_to_all(spatial, 'seq', 1, 2, tiled=True)  189 us
    all_to_all x1, blocking collectives, per_device(): by_channel = lax.all_to_all(gate_n, 'seq', 2, 1, tiled=True)  151 us
    convert_element_type x2, local copies, waits for them, and re-layouts, per_device(): by_patch.astype(jnp.float32) + local_bias[:, None]  38.2 us
    dot_general x1, matrix products, per_device(): jnp.einsum('bse,ec->bsc', gated, w_out, preferred_element_type=jnp.float32)  36.8 us
    unnamed x18, local copies, waits for them, and re-layouts  33 us
    dot_general x1, matrix products, gelu_proj(): jnp.einsum('bsc,cf->bsf', normed, weight, preferred_element_type=jnp.floa...  32.6 us
    all_to_all x1, local copies, waits for them, and re-layouts, per_device(): by_channel = lax.all_to_all(gate_n, 'seq', 2, 1, tiled=True)  23.1 us
    convert_element_type x1, local copies, waits for them, and re-layouts, layer_norm(): (centered * lax.rsqrt(var_val + LN_EPS) * gain_vec + offset).astype(jnp.b...  22.5 us
  transfers between devices with their start and end apart: 1, of which 1 were waited for; matrix products, arithmetic and copies ran while one was open for 0% of the time, Pallas kernels for 0%

commit v1 on v0

v1 whole, which is shorter than its diff:
```python
import jax
import jax.numpy as jnp
from jax import lax
from jax.sharding import PartitionSpec as P

LN_EPS = 1e-6


def layer_norm(values, gain_vec, offset):
    values_f = values.astype(jnp.float32)
    mean_val = jnp.mean(values_f, axis=-1, keepdims=True)
    centered = values_f - mean_val
    var_val = jnp.mean(centered * centered, axis=-1, keepdims=True)
    return (centered * lax.rsqrt(var_val + LN_EPS) * gain_vec + offset).astype(jnp.bfloat16)


def gelu_proj(normed, weight, offset):
    hidden = jnp.einsum("bsc,cf->bsf", normed, weight, preferred_element_type=jnp.float32) + offset
    return jax.nn.gelu(hidden, approximate=False).astype(jnp.bfloat16)


def solution(mesh):
    row_spec = P("data", "seq", None)
    vec_spec = P(None)
    mat_spec = P(None, None)
    in_specs = (row_spec, vec_spec, vec_spec, mat_spec, vec_spec, vec_spec, vec_spec, mat_spec, vec_spec, mat_spec, vec_spec)

    def per_device(patches, ln1_gain, ln1_bias, w_in, b_in, ln2_gain, ln2_bias, w_spatial, b_spatial, w_out, b_out):
        half_dim = w_out.shape[0]
        images = lax.all_to_all(patches, "seq", 0, 1, tiled=True)
        normed = layer_norm(images, ln1_gain, ln1_bias)
        gate_a = gelu_proj(normed, w_in[:, :half_dim], b_in[:half_dim])
        gate_n = layer_norm(gelu_proj(normed, w_in[:, half_dim:], b_in[half_dim:]), ln2_gain, ln2_bias)
        spatial = jnp.einsum("rs,bre->bse", w_spatial, gate_n, preferred_element_type=jnp.float32).astype(jnp.bfloat16)
        gated = (gate_a.astype(jnp.float32) * (spatial.astype(jnp.float32) + b_spatial[:, None])).astype(jnp.bfloat16)
        mixed = jnp.einsum("bse,ec->bsc", gated, w_out, preferred_element_type=jnp.float32) + b_out
        result = (images.astype(jnp.float32) + mixed).astype(jnp.bfloat16)
        return lax.all_to_all(result, "seq", 1, 0, tiled=True)

    return jax.shard_map(per_device, mesh=mesh, in_specs=in_specs, out_specs=row_spec, check_vma=False)
```

time: 601 us -> 209 us (0.35); the launches traced: 590 us -> 209 us
  waiting for transfers between devices: 189 us -> 48 us
  local copies, waits for them, and re-layouts: 142 us -> 6.83 us
  blocking collectives: 151 us -> 55.9 us
  matrix products: 79.5 us -> 49.8 us
  other arithmetic: 22.4 us -> 37 us
    all_to_all x1, waiting for transfers between devices: 189 us -> 48 us  [per_device(): images = lax.all_to_all(patches, 'seq', 0, 1, tiled=True)]
    all_to_all x1, blocking collectives: 151 us -> 55.9 us  [per_device(): return lax.all_to_all(result, 'seq', 1, 0, tiled=True)]
    convert_element_type x4 -> x2, local copies, waits for them, and re-layouts: 72.2 us -> 3.95 us  [per_device(): result = (images.astype(jnp.float32) + mixed).astype(jnp.bfloat16)]
    all_to_all x2 -> x1, local copies, waits for them, and re-layouts: 35 us -> 1.9 us  [per_device(): return lax.all_to_all(result, 'seq', 1, 0, tiled=True)]
    unnamed x18, local copies, waits for them, and re-layouts: 33 us -> 0.05 us
    dot_general x1, matrix products: 36.8 us -> 4.11 us  [per_device(): jnp.einsum('bse,ec->bsc', gated, w_out, preferred_element_type=jnp.float32)]
    reduce_sum x1 -> x2, other arithmetic: 2.06 us -> 31.2 us  [layer_norm(): mean_val = jnp.mean(values_f, axis=-1, keepdims=True)]
    dot_general x1, matrix products: 10 us -> 34.2 us  [per_device(): jnp.einsum('rs,bre->bse', w_spatial, gate_n, preferred_element_type=jnp.f...]
where the time goes in v1:
time: 209 us
  blocking collectives  55.9 us (27%)
  matrix products  49.8 us (24%)
  waiting for transfers between devices  48 us (23%)
  other arithmetic  37 us (18%)
  starting transfers between devices  10.9 us (5%)
  local copies, waits for them, and re-layouts  6.83 us (3%)
    all_to_all x1, blocking collectives, per_device(): return lax.all_to_all(result, 'seq', 1, 0, tiled=True)  55.9 us
    all_to_all x1, waiting for transfers between devices, per_device(): images = lax.all_to_all(patches, 'seq', 0, 1, tiled=True)  48 us
    dot_general x1, matrix products, per_device(): jnp.einsum('rs,bre->bse', w_spatial, gate_n, preferred_element_type=jnp.f...  34.2 us
    reduce_sum x2, other arithmetic, layer_norm(): mean_val = jnp.mean(values_f, axis=-1, keepdims=True)  31.2 us
    dot_general x2, matrix products, gelu_proj(): jnp.einsum('bsc,cf->bsf', normed, weight, preferred_element_type=jnp.floa...  11.6 us
    all_to_all x1, starting transfers between devices, per_device(): images = lax.all_to_all(patches, 'seq', 0, 1, tiled=True)  10.9 us
  transfers between devices with their start and end apart: 1, of which 1 were waited for; matrix products, arithmetic and copies ran while one was open for 0% of the time, Pallas kernels for 0%

profile of v1, /device:TPU:21, one launch (start us, length us, event | category | flops | bytes accessed | tf_op | source)
XLA Modules:
  0.0 208.7 jit_solution(17885971859319606346)
XLA Ops:
  0.0 10.9 %all-to-all-start = ((bf16[64,32,512]{2,1,0:T(8,128)(2,1)}), bf16[64,32,512]{2,1,0:T(8,128)(2,1)}, u32[]{:S(2)}, u32[]{:S(2)}) async-start(bf16[64,32,512]{2,1,0:T(8,128)(2,1)} %param.11), calls=%async_computation | async-start | bytes 4194304 | tf_op jit(solution)/shard_map/all_to_all | solution.py:30
  10.9 0.8 fusion.128
  11.7 48.0 %all-to-all-done = bf16[64,32,512]{2,1,0:T(8,128)(2,1)} async-done(((bf16[64,32,512]{2,1,0:T(8,128)(2,1)}), bf16[64,32,512]{2,1,0:T(8,128)(2,1)}, u32[]{:S(2)}, u32[]{:S(2)}) %all-to-all-start) | async-done | bytes 2097184 | tf_op jit(solution)/shard_map/all_to_all | solution.py:30
  59.7 2.2 %bitcast_convert_fusion = f32[16,4,32,512]{3,2,1,0:T(8,128)S(1)} fusion(bf16[64,32,512]{2,1,0:T(8,128)(2,1)} %all-to-all-done), kind=kLoop, calls=%fused_computation.142 | loop fusion | flops 1048576 | bytes 6291456 | tf_op jit(solution)/shard_map/convert_element_type | solution.py:37
  61.9 0.4 bitcast_reduce_fusion
  62.3 0.7 fusion.82
  63.0 0.1 div.15
  63.1 0.1 rsqrt.20
  63.1 2.3 %copy.14 = f32[16,4,32,512]{3,2,0,1:T(8,128)S(1)} copy(bf16[16,4,32,512]{3,2,1,0:T(8,128)(2,1)} %bitcast.12) | data formatting | bytes 6291456 | tf_op jit(solution)/shard_map/convert_element_type | solution.py:37
  65.5 1.1 fusion.79
  66.6 6.5 %fusion.91 = f32[4,512,1536]{2,1,0:T(8,128)} fusion(bf16[4,512,512]{2,1,0:T(8,128)(2,1)S(1)} %fusion.79, bf16[512,3072]{1,0:T(8,128)(2,1)S(1)} %copy-done.3), kind=kOutput, calls=%fused_computation.102 | convolution fusion | flops 3221225472 | bytes 16252928 | tf_op jit(solution)/shard_map/bsc,cf->bsf/dot_general | solution.py:18
  73.1 5.1 %fusion.83 = (u8[512,1536]{1,0:T(8,128)(4,1)S(1)}, f32[4,512,1536]{2,1,0:T(8,128)S(1)}) fusion(f32[1536]{0:T(1024)S(1)} %get-tuple-element.8, bf16[4,512,512]{2,1,0:T(8,128)(2,1)S(1)} %fusion.79, bf16[512,3072]{1,0:T(8,128)(2,1)S(1)} %copy-done.3), kind=kOutput, calls=%fused_computation.98 | convolution fusion | flops 3248750592 | bytes 17047552 | tf_op jit(solution)/shard_map/bsc,cf->bsf/dot_general | solution.py:18
  78.2 0.0 copy-start.4
  78.2 0.0 copy-start.5
  78.2 0.0 copy-start.6
  78.2 0.0 copy-start.7
  78.2 30.8 %convert_reduce_fusion = (f32[4,512]{1,0:T(4,128)S(1)}, bf16[4,512,1536]{2,1,0:T(8,128)(2,1)S(1)}) fusion(u8[512,1536]{1,0:T(8,128)(4,1)S(1)} %get-tuple-element.9, f32[4,512,1536]{2,1,0:T(8,128)S(1)} %get-tuple-element.10, f32[1536]{0:T(1024)S(1)} %get-tuple-element.8), kind=kLoop, calls=%fused_computation.3 | loop fusion | flops 223344640 | bytes 19675136 | tf_op jit(solution)/shard_map/reduce_sum | solution.py:11
  109.1 1.8 fusion.2
  110.9 0.0 copy-start.8
  111.0 34.2 %fusion.140 = bf16[4,512,1536]{2,1,0:T(8,128)(2,1)S(1)} fusion(f32[4,512,1536]{2,1,0:T(8,128)} %fusion.91, f32[512]{0:T(512)S(1)} %copy-done.7, bf16[4,512,1536]{2,1,0:T(8,128)(2,1)S(1)} %get-tuple-element.6, f32[1536]{0:T(1024)S(1)} %copy-done.5, f32[1536]{0:T(1024)S(1)} %copy-done.6, f32[4,512]{1,0:T(4,128)S(1)} %add_rsqrt_fusion.1, ...), kind=kOutput, calls=%fused_computation.19.clone.clone.clone.clone.1 | convolution fusion | flops 3466592256 | bytes 25726976 | tf_op jit(solution)/shard_map/rs,bre->bse/dot_general | solution.py:34
  145.2 4.1 %fusion.80 = bf16[4,512,512]{2,1,0:T(8,128)(2,1)S(1)} fusion(f32[16,4,32,512]{3,2,0,1:T(8,128)S(1)} %copy.14, f32[512]{0:T(512)S(1)} %copy-done.8, bf16[1536,512]{1,0:T(8,128)(2,1)S(1)} %copy-done, bf16[4,512,1536]{2,1,0:T(8,128)(2,1)S(1)} %fusion.140), kind=kOutput, calls=%fused_computation.93 | convolution fusion | flops 3224371200 | bytes 14157824 | tf_op jit(solution)/shard_map/bse,ec->bsc/dot_general | solution.py:36
  149.3 1.6 copy.15
  150.9 55.9 %all_to_all.27 = bf16[4,512,512]{2,0,1:T(4,128)(2,1)S(1)} all-to-all(bf16[4,512,512]{2,0,1:T(4,128)(2,1)S(1)} %copy.15), channel_id=1, replica_groups=mesh['data'=4,'seq'=16] {'seq'}, dimensions={1} | all-to-all | bytes 4194304 | tf_op jit(solution)/shard_map/all_to_all | solution.py:38
  206.8 1.9 copy.16
  (17 shorter events, 0.1 us)
Async XLA Ops:
  0.0 145.1 %copy-start = (bf16[1536,512]{1,0:T(8,128)(2,1)S(1)}, bf16[1536,512]{1,0:T(8,128)(2,1)}, u32[]{:S(2)}) copy-start(bf16[1536,512]{1,0:T(8,128)(2,1)} %param.20) | copy-start | bytes 4718596
  0.0 65.5 %copy-start.2 = (f32[512]{0:T(512)S(1)}, f32[512]{0:T(512)}, u32[]{:S(2)}) copy-start(f32[512]{0:T(512)} %param.12) | copy-start | bytes 6148
  0.0 65.5 %copy-start.1 = (f32[512]{0:T(512)S(1)}, f32[512]{0:T(512)}, u32[]{:S(2)}) copy-start(f32[512]{0:T(512)} %param.13) | copy-start | bytes 6148
  0.0 59.7 %all-to-all-start = ((bf16[64,32,512]{2,1,0:T(8,128)(2,1)}), bf16[64,32,512]{2,1,0:T(8,128)(2,1)}, u32[]{:S(2)}, u32[]{:S(2)}) async-start(bf16[64,32,512]{2,1,0:T(8,128)(2,1)} %param.11), calls=%async_computation | async-start | bytes 4194304 | tf_op jit(solution)/shard_map/all_to_all | solution.py:30
  63.1 3.5 %copy-start.3 = (bf16[512,3072]{1,0:T(8,128)(2,1)S(1)}, bf16[512,3072]{1,0:T(8,128)(2,1)}, u32[]{:S(2)}) copy-start(bf16[512,3072]{1,0:T(8,128)(2,1)} %param.14) | copy-start | bytes 9437188
  78.2 32.7 %copy-start.4 = (bf16[512,512]{1,0:T(8,128)(2,1)S(1)}, bf16[512,512]{1,0:T(8,128)(2,1)}, u32[]{:S(2)}) copy-start(bf16[512,512]{1,0:T(8,128)(2,1)} %param.18) | copy-start | bytes 1572868
  78.2 32.7 %copy-start.5 = (f32[1536]{0:T(1024)S(1)}, f32[1536]{0:T(1024)}, u32[]{:S(2)}) copy-start(f32[1536]{0:T(1024)} %param.17) | copy-start | bytes 18436
  78.2 32.7 %copy-start.6 = (f32[1536]{0:T(1024)S(1)}, f32[1536]{0:T(1024)}, u32[]{:S(2)}) copy-start(f32[1536]{0:T(1024)} %param.16) | copy-start | bytes 18436
  78.2 32.7 %copy-start.7 = (f32[512]{0:T(512)S(1)}, f32[512]{0:T(512)}, u32[]{:S(2)}) copy-start(f32[512]{0:T(512)} %param.19) | copy-start | bytes 6148
  110.9 34.2 %copy-start.8 = (f32[512]{0:T(512)S(1)}, f32[512]{0:T(512)}, u32[]{:S(2)}) copy-start(f32[512]{0:T(512)} %param.21) | copy-start | bytes 6148

commit v2 on v1

v2 whole, which is shorter than its diff:
```python
import functools

import jax
import jax.numpy as jnp
from jax import lax
from jax.experimental import pallas as pl
from jax.experimental.pallas import tpu as pltpu
from jax.sharding import PartitionSpec as P

LN_EPS = 1e-6
MESH = pl.DeviceIdType.MESH
SQRT_HALF = 0.7071067811865476


def normalize(values_f, gain_vec, offset):
    mean_val = jnp.mean(values_f, axis=-1, keepdims=True)
    centered = values_f - mean_val
    var_val = jnp.mean(centered * centered, axis=-1, keepdims=True)
    return (centered * lax.rsqrt(var_val + LN_EPS) * gain_vec + offset).astype(jnp.bfloat16)


def kernel(n, row_tile, col_tile, x_hbm, g1_hbm, b1_hbm, wi_hbm, bi_hbm, g2_hbm, b2_hbm, ws_hbm, bs_hbm, wo_hbm, bo_hbm,
           out_hbm, gath, ybuf, hbuf, nbuf, gbuf, g1, b1, wi, bi, g2, b2, ws, wst, bs, bst, wo, bo,
           w_sem, in_send, in_recv, out_send, out_recv):
    me = lax.axis_index("seq")
    per_dev, rows, chans = x_hbm.shape[1], x_hbm.shape[2], x_hbm.shape[3]
    patches = n * rows
    half = wo.shape[0]
    bf16, f32 = jnp.bfloat16, jnp.float32

    def partner(k):
        step = lax.div(k + 1, 2) * (2 * lax.rem(k, 2) - 1)
        return lax.rem(me + step + n, n)

    loads = [pltpu.make_async_copy(src, dst, w_sem.at[i]) for i, (src, dst) in enumerate((
        (g1_hbm, g1), (b1_hbm, b1), (wi_hbm, wi), (bi_hbm, bi), (g2_hbm, g2), (b2_hbm, b2),
        (ws_hbm, ws), (bs_hbm, bs), (wo_hbm, wo), (bo_hbm, bo)))]
    for load in loads:
        load.start()

    barrier = pltpu.get_barrier_semaphore()

    def greet(k, carry):
        pl.semaphore_signal(barrier, inc=1, device_id={"seq": partner(k)}, device_id_type=MESH)
        return carry

    lax.fori_loop(1, n, greet, 0)
    pl.semaphore_wait(barrier, n - 1)

    def mine(base):
        return pl.ds(pl.multiple_of(base * patches + me * rows, rows), rows)

    def send_in(i, carry):
        j, k = lax.div(i, n - 1), lax.rem(i, n - 1) + 1
        to = partner(k)
        pltpu.make_async_remote_copy(
            src_ref=x_hbm.at[to, j], dst_ref=gath.at[mine(j)], send_sem=in_send.at[0], recv_sem=in_recv.at[j],
            device_id={"seq": to}, device_id_type=MESH).start()
        return carry

    lax.fori_loop(0, per_dev * (n - 1), send_in, 0)
    for j in range(per_dev):
        pltpu.make_async_copy(x_hbm.at[me, j], gath.at[mine(j)], in_recv.at[j]).start()

    for load in loads:
        load.wait()
    wst[...] = jnp.transpose(ws[...].astype(f32)).astype(bf16)
    bst[...] = jnp.transpose(jnp.broadcast_to(bs[...], (128, patches)))

    def one_image(j, carry):
        base = pl.multiple_of(j * patches, patches)
        image = gath.at[pl.ds(base, patches)]
        pltpu.make_async_copy(image, image, in_recv.at[j]).wait()

        def project(r, carry):
            start = pl.multiple_of(r * row_tile, row_tile)
            sl = pl.ds(start, row_tile)
            u = normalize(gath[pl.ds(pl.multiple_of(base + start, row_tile), row_tile), :].astype(f32), g1[...], b1[...])

            def column(c, carry):
                cs = pl.ds(pl.multiple_of(c * col_tile, col_tile), col_tile)
                hidden = jnp.dot(u, wi[:, cs], preferred_element_type=f32) + bi[:, cs]
                hbuf[sl, cs] = (0.5 * hidden * (1.0 + lax.erf(hidden * SQRT_HALF))).astype(bf16)
                return carry

            lax.fori_loop(0, 2 * half // col_tile, column, 0)

            def norm2(q, carry):
                qs = pl.ds(pl.multiple_of(start + q * 32, 32), 32)
                nbuf[qs, :] = normalize(hbuf[qs, half:].astype(f32), g2[...], b2[...])
                return carry

            lax.fori_loop(0, row_tile // 32, norm2, 0)
            return carry

        lax.fori_loop(0, patches // row_tile, project, 0)

        def mix(r, carry):
            start = pl.multiple_of(r * row_tile, row_tile)
            sl = pl.ds(start, row_tile)
            ysl = pl.ds(pl.multiple_of(base + start, row_tile), row_tile)
            bias = jnp.concatenate([bst[sl, :]] * (col_tile // 128), axis=1)

            def column(c, carry):
                cs = pl.ds(pl.multiple_of(c * col_tile, col_tile), col_tile)
                s = jnp.dot(wst[sl, :], nbuf[:, cs], preferred_element_type=f32).astype(bf16).astype(f32)
                gbuf[:, cs] = (hbuf[sl, cs].astype(f32) * (s + bias)).astype(bf16)
                return carry

            lax.fori_loop(0, half // col_tile, column, 0)
            mixed = jnp.dot(gbuf[...], wo[...], preferred_element_type=f32) + bo[...]
            ybuf[ysl, :] = (gath[ysl, :].astype(f32) + mixed).astype(bf16)
            return carry

        lax.fori_loop(0, patches // row_tile, mix, 0)

        def rows_of(dev):
            return pl.ds(pl.multiple_of(base + dev * rows, rows), rows)

        def send_out(k, carry):
            to = partner(k)
            pltpu.make_async_remote_copy(
                src_ref=ybuf.at[rows_of(to)], dst_ref=out_hbm.at[me, j], send_sem=out_send.at[0], recv_sem=out_recv.at[0],
                device_id={"seq": to}, device_id_type=MESH).start()
            return carry

        lax.fori_loop(1, n, send_out, 0)
        pltpu.make_async_copy(ybuf.at[rows_of(me)], out_hbm.at[me, j], out_recv.at[0]).start()
        return carry

    lax.fori_loop(0, per_dev, one_image, 0)

    sent = pl.ds(0, per_dev * (n - 1) * rows)
    pltpu.make_async_copy(ybuf.at[sent], ybuf.at[sent], in_send.at[0]).wait()
    pltpu.make_async_copy(ybuf.at[sent], ybuf.at[sent], out_send.at[0]).wait()
    pltpu.make_async_copy(out_hbm, out_hbm, out_recv.at[0]).wait()


def solution(mesh):
    row_spec = P("data", "seq", None)
    vec_spec = P(None)
    mat_spec = P(None, None)
    in_specs = (row_spec, vec_spec, vec_spec, mat_spec, vec_spec, vec_spec, vec_spec, mat_spec, vec_spec, mat_spec, vec_spec)
    n = mesh.shape["seq"]

    def per_device(patches, ln1_gain, ln1_bias, w_in, b_in, ln2_gain, ln2_bias, w_spatial, b_spatial, w_out, b_out):
        images, rows, chans = patches.shape
        half = w_out.shape[0]
        per_dev = images // n
        total = n * rows
        row_tile, col_tile = 256, 512
        bf16, f32 = jnp.bfloat16, jnp.float32
        dma, vmem = pltpu.SemaphoreType.DMA, pltpu.VMEM
        out = pl.pallas_call(
            functools.partial(kernel, n, row_tile, col_tile),
            out_shape=jax.ShapeDtypeStruct((n, per_dev, rows, chans), bf16),
            in_specs=[pl.BlockSpec(memory_space=pltpu.HBM)] * 11,
            out_specs=pl.BlockSpec(memory_space=pltpu.HBM),
            scratch_shapes=[
                vmem((per_dev * total, chans), bf16),
                vmem((per_dev * total, chans), bf16),
                vmem((total, 2 * half), bf16),
                vmem((total, half), bf16),
                vmem((row_tile, half), bf16),
                vmem((1, chans), f32), vmem((1, chans), f32),
                vmem((chans, 2 * half), bf16), vmem((1, 2 * half), f32),
                vmem((1, half), f32), vmem((1, half), f32),
                vmem((total, total), bf16), vmem((total, total), bf16),
                vmem((1, total), f32), vmem((total, 128), f32),
                vmem((half, chans), bf16), vmem((1, chans), f32),
                dma((10,)), dma((1,)), dma((per_dev,)), dma((1,)), dma((1,)),
            ],
            compiler_params=pltpu.CompilerParams(
                collective_id=0, has_side_effects=True, vmem_limit_bytes=56 * 1024 * 1024),
            name="gmlp",
        )(patches.reshape(n, per_dev, rows, chans), ln1_gain[None], ln1_bias[None], w_in, b_in[None],
          ln2_gain[None], ln2_bias[None], w_spatial, b_spatial[None], w_out, b_out[None])
        return out.reshape(images, rows, chans)

    return jax.shard_map(per_device, mesh=mesh, in_specs=in_specs, out_specs=row_spec, check_vma=False)
```

time: 209 us -> 107 us (0.51)
  Pallas kernels: 0 us -> 100 us
  blocking collectives: 55.9 us -> 0 us
  matrix products: 49.8 us -> 0 us
  waiting for transfers between devices: 48 us -> 0 us
  other arithmetic: 37 us -> 0 us
  starting transfers between devices: 10.9 us -> 0 us
    pallas_call x0 -> x1, Pallas kernels: none -> 100 us  [per_device(): pl.pallas_call(functools.partial(kernel, n, row_tile, col_tile), out_shap...]
    all_to_all x1 -> x0, blocking collectives: 55.9 us -> none  [per_device(): return lax.all_to_all(result, 'seq', 1, 0, tiled=True)]
    dot_general x4 -> x0, matrix products: 49.8 us -> none  [the longest x1 34.2 us: per_device(): jnp.einsum('rs,bre->bse', w_spatial, gate_n, preferred_element_type=jnp.f...]
    all_to_all x1 -> x0, waiting for transfers between devices: 48 us -> none  [per_device(): images = lax.all_to_all(patches, 'seq', 0, 1, tiled=True)]
    reduce_sum x4 -> x0, other arithmetic: 33.7 us -> none  [the longest x2 31.2 us: layer_norm(): mean_val = jnp.mean(values_f, axis=-1, keepdims=True)]
    all_to_all x1 -> x0, starting transfers between devices: 10.9 us -> none  [per_device(): images = lax.all_to_all(patches, 'seq', 0, 1, tiled=True)]
    convert_element_type x2 -> x0, local copies, waits for them, and re-layouts: 3.95 us -> none  [per_device(): result = (images.astype(jnp.float32) + mixed).astype(jnp.bfloat16)]
    convert_element_type x2 -> x0, other arithmetic: 3.3 us -> none  [the longest x1 2.19 us: per_device(): result = (images.astype(jnp.float32) + mixed).astype(jnp.bfloat16)]
  transfers between devices with their start and end apart: 1 -> 0, of which waited for: 1 -> 0; matrix products, arithmetic and copies ran while one was open for 0% -> 0% of each run, Pallas kernels for 0% -> 0%
where the time goes in v2:
time: 107 us; the launch traced here: 106 us
  Pallas kernels  100 us (93%)
  local copies, waits for them, and re-layouts  5.75 us (5%)
    pallas_call x1, Pallas kernels, per_device(): pl.pallas_call(functools.partial(kernel, n, row_tile, col_tile), out_shap...  100 us
    unnamed x1, local copies, waits for them, and re-layouts  3.16 us

profile of v2, /device:TPU:21, one launch (start us, length us, event | category | flops | bytes accessed | tf_op | source)
XLA Modules:
  0.0 105.9 jit_solution(10269889367241143475)
XLA Ops:
  0.0 1.3 %broadcast_in_dim.24.g2_hbm = f32[1,1536]{1,0:T(1,128)} reshape(f32[1536]{0:T(1024)} %param.16) | data formatting | bytes 12288 | tf_op jit(solution)/shard_map/broadcast_in_dim | solution.py:177
  1.3 1.3 %broadcast_in_dim.25.b2_hbm = f32[1,1536]{1,0:T(1,128)} reshape(f32[1536]{0:T(1024)} %param.17) | data formatting | bytes 12288 | tf_op jit(solution)/shard_map/broadcast_in_dim | solution.py:177
  2.6 100.1 %gmlp.1 = bf16[16,4,32,512]{3,2,1,0:T(8,128)(2,1)} custom-call(bf16[16,4,32,512]{3,2,1,0:T(8,128)(2,1)} %bitcast.8, f32[1,512]{1,0:T(1,128)} %bitcast.10, f32[1,512]{1,0:T(1,128)} %bitcast.11, bf16[512,3072]{1,0:T(8,128)(2,1)} %wi_hbm.1, f32[1,3072]{1,0:T(1,128)} %bitcast.9, f32[1,1536]{1,0:T(1,128)} %broadcast_in_dim.24.g2_hbm, ...), custom_call_target="tpu_custom_call" | custom-call | tf_op jit(solution)/shard_map/gmlp/pallas_call | solution.py:154
  102.7 3.2 %copy.13 = bf16[64,32,512]{2,1,0:T(8,128)(2,1)} copy(bf16[64,32,512]{2,1,0:T(8,128)(2,1)} %bitcast.7) | data formatting | bytes 4194304

commit v3 on v2

--- a/solution.py
+++ b/solution.py
@@ -20,7 +20,7 @@
 
 
 def kernel(n, row_tile, col_tile, x_hbm, g1_hbm, b1_hbm, wi_hbm, bi_hbm, g2_hbm, b2_hbm, ws_hbm, bs_hbm, wo_hbm, bo_hbm,
-           out_hbm, gath, ybuf, hbuf, nbuf, gbuf, g1, b1, wi, bi, g2, b2, ws, wst, bs, bst, wo, bo,
+           out_ref, gath, ybuf, hbuf, nbuf, gbuf, g1, b1, wi, bi, g2, b2, ws, wst, bs, bst, wo, bo,
            w_sem, in_send, in_recv, out_send, out_recv):
     me = lax.axis_index("seq")
     per_dev, rows, chans = x_hbm.shape[1], x_hbm.shape[2], x_hbm.shape[3]
@@ -28,9 +28,19 @@
     half = wo.shape[0]
     bf16, f32 = jnp.bfloat16, jnp.float32
 
-    def partner(k):
-        step = lax.div(k + 1, 2) * (2 * lax.rem(k, 2) - 1)
-        return lax.rem(me + step + n, n)
+    chips = n // 2
+    chip, core = lax.div(me, 2), lax.rem(me, 2)
+
+    def others(steps):
+        found = []
+        for step in steps:
+            there = 2 * lax.rem(chip + step + chips, chips)
+            found += [there + core, there + 1 - core]
+        return found + [2 * chip + 1 - core]
+
+    pairs = [(step, -step) for step in range(chips // 2 - 1, 0, -1)]
+    out_steps = [chips // 2, *sum(pairs, ())]
+    in_steps = [chips // 2, *sum(pairs[-1:] + pairs[:-1], ())]
 
     loads = [pltpu.make_async_copy(src, dst, w_sem.at[i]) for i, (src, dst) in enumerate((
         (g1_hbm, g1), (b1_hbm, b1), (wi_hbm, wi), (bi_hbm, bi), (g2_hbm, g2), (b2_hbm, b2),
@@ -40,25 +50,21 @@
 
     barrier = pltpu.get_barrier_semaphore()
 
-    def greet(k, carry):
-        pl.semaphore_signal(barrier, inc=1, device_id={"seq": partner(k)}, device_id_type=MESH)
-        return carry
-
-    lax.fori_loop(1, n, greet, 0)
+    for to in others(in_steps):
+        pl.semaphore_signal(barrier, inc=1, device_id={"seq": to}, device_id_type=MESH)
     pl.semaphore_wait(barrier, n - 1)
 
     def mine(base):
         return pl.ds(pl.multiple_of(base * patches + me * rows, rows), rows)
 
-    def send_in(i, carry):
-        j, k = lax.div(i, n - 1), lax.rem(i, n - 1) + 1
-        to = partner(k)
-        pltpu.make_async_remote_copy(
-            src_ref=x_hbm.at[to, j], dst_ref=gath.at[mine(j)], send_sem=in_send.at[0], recv_sem=in_recv.at[j],
-            device_id={"seq": to}, device_id_type=MESH).start()
+    def send_in(j, carry):
+        for to in others(in_steps):
+            pltpu.make_async_remote_copy(
+                src_ref=x_hbm.at[to, j], dst_ref=gath.at[mine(j)], send_sem=in_send.at[0], recv_sem=in_recv.at[j],
+                device_id={"seq": to}, device_id_type=MESH).start()
         return carry
 
-    lax.fori_loop(0, per_dev * (n - 1), send_in, 0)
+    lax.fori_loop(0, per_dev, send_in, 0)
     for j in range(per_dev):
         pltpu.make_async_copy(x_hbm.at[me, j], gath.at[mine(j)], in_recv.at[j]).start()
 
@@ -87,7 +93,7 @@
 
             def norm2(q, carry):
                 qs = pl.ds(pl.multiple_of(start + q * 32, 32), 32)
-                nbuf[qs, :] = normalize(hbuf[qs, half:].astype(f32), g2[...], b2[...])
+                nbuf[qs, :] = normalize(hbuf[qs, half:].astype(f32), g2[...].reshape(1, half), b2[...].reshape(1, half))
                 return carry
 
             lax.fori_loop(0, row_tile // 32, norm2, 0)
@@ -117,15 +123,11 @@
         def rows_of(dev):
             return pl.ds(pl.multiple_of(base + dev * rows, rows), rows)
 
-        def send_out(k, carry):
-            to = partner(k)
+        for to in others(out_steps):
             pltpu.make_async_remote_copy(
-                src_ref=ybuf.at[rows_of(to)], dst_ref=out_hbm.at[me, j], send_sem=out_send.at[0], recv_sem=out_recv.at[0],
+                src_ref=ybuf.at[rows_of(to)], dst_ref=out_ref.at[me, j], send_sem=out_send.at[0], recv_sem=out_recv.at[0],
                 device_id={"seq": to}, device_id_type=MESH).start()
-            return carry
-
-        lax.fori_loop(1, n, send_out, 0)
-        pltpu.make_async_copy(ybuf.at[rows_of(me)], out_hbm.at[me, j], out_recv.at[0]).start()
+        pltpu.make_async_copy(ybuf.at[rows_of(me)], out_ref.at[me, j], out_recv.at[0]).start()
         return carry
 
     lax.fori_loop(0, per_dev, one_image, 0)
@@ -133,7 +135,7 @@
     sent = pl.ds(0, per_dev * (n - 1) * rows)
     pltpu.make_async_copy(ybuf.at[sent], ybuf.at[sent], in_send.at[0]).wait()
     pltpu.make_async_copy(ybuf.at[sent], ybuf.at[sent], out_send.at[0]).wait()
-    pltpu.make_async_copy(out_hbm, out_hbm, out_recv.at[0]).wait()
+    pltpu.make_async_copy(out_ref, out_ref, out_recv.at[0]).wait()
 
 
 def solution(mesh):
@@ -153,9 +155,9 @@
         dma, vmem = pltpu.SemaphoreType.DMA, pltpu.VMEM
         out = pl.pallas_call(
             functools.partial(kernel, n, row_tile, col_tile),
-            out_shape=jax.ShapeDtypeStruct((n, per_dev, rows, chans), bf16),
+            out_shape=pltpu.VMEM((n, per_dev, rows, chans), bf16),
             in_specs=[pl.BlockSpec(memory_space=pltpu.HBM)] * 11,
-            out_specs=pl.BlockSpec(memory_space=pltpu.HBM),
+            out_specs=pl.BlockSpec(memory_space=pltpu.VMEM),
             scratch_shapes=[
                 vmem((per_dev * total, chans), bf16),
                 vmem((per_dev * total, chans), bf16),
@@ -164,7 +166,7 @@
                 vmem((row_tile, half), bf16),
                 vmem((1, chans), f32), vmem((1, chans), f32),
                 vmem((chans, 2 * half), bf16), vmem((1, 2 * half), f32),
-                vmem((1, half), f32), vmem((1, half), f32),
+                vmem((half,), f32), vmem((half,), f32),
                 vmem((total, total), bf16), vmem((total, total), bf16),
                 vmem((1, total), f32), vmem((total, 128), f32),
                 vmem((half, chans), bf16), vmem((1, chans), f32),
@@ -174,7 +176,7 @@
                 collective_id=0, has_side_effects=True, vmem_limit_bytes=56 * 1024 * 1024),
             name="gmlp",
         )(patches.reshape(n, per_dev, rows, chans), ln1_gain[None], ln1_bias[None], w_in, b_in[None],
-          ln2_gain[None], ln2_bias[None], w_spatial, b_spatial[None], w_out, b_out[None])
+          ln2_gain, ln2_bias, w_spatial, b_spatial[None], w_out, b_out[None])
         return out.reshape(images, rows, chans)
 
     return jax.shard_map(per_device, mesh=mesh, in_specs=in_specs, out_specs=row_spec, check_vma=False)

time: 107 us -> 101 us (0.944); the launches traced: 106 us -> 101 us
  local copies, waits for them, and re-layouts: 5.75 us -> 1.32 us
    broadcast_in_dim x2 -> x0, local copies, waits for them, and re-layouts: 2.59 us -> none  [the longest x1 1.3 us: per_device(): ln2_bias[None]]
    unnamed x1, local copies, waits for them, and re-layouts: 3.16 us -> 1.32 us
where the time goes in v3:
time: 101 us
  Pallas kernels  100 us (99%)
  local copies, waits for them, and re-layouts  1.32 us (1%)
    pallas_call x1, Pallas kernels, per_device(): pl.pallas_call(functools.partial(kernel, n, row_tile, col_tile), out_shap...  100 us

profile of v3, /device:TPU:21, one launch (start us, length us, event | category | flops | bytes accessed | tf_op | source)
XLA Modules:
  0.0 101.4 jit_solution(819264741083690083)
XLA Ops:
  0.0 100.1 %gmlp.1 = bf16[16,4,32,512]{3,2,1,0:T(8,128)(2,1)S(1)} custom-call(bf16[16,4,32,512]{3,2,1,0:T(8,128)(2,1)} %bitcast.8, f32[1,512]{1,0:T(1,128)} %bitcast.10, f32[1,512]{1,0:T(1,128)} %bitcast.11, bf16[512,3072]{1,0:T(8,128)(2,1)} %wi_hbm.1, f32[1,3072]{1,0:T(1,128)} %bitcast.9, f32[1536]{0:T(1024)} %g2_hbm.1, f32[1536]{0:T(1024)} %b2_hbm.1, ...), custom_call_target="tpu_custom_call" | custom-call | tf_op jit(solution)/shard_map/gmlp/pallas_call | solution.py:156
  100.1 1.3 %copy.13 = bf16[64,32,512]{2,1,0:T(8,128)(2,1)} copy(bf16[64,32,512]{2,1,0:T(8,128)(2,1)S(1)} %bitcast.7) | data formatting | bytes 4194304

commit v4 on v3

--- a/solution.py
+++ b/solution.py
@@ -28,19 +28,9 @@
     half = wo.shape[0]
     bf16, f32 = jnp.bfloat16, jnp.float32
 
-    chips = n // 2
-    chip, core = lax.div(me, 2), lax.rem(me, 2)
-
-    def others(steps):
-        found = []
-        for step in steps:
-            there = 2 * lax.rem(chip + step + chips, chips)
-            found += [there + core, there + 1 - core]
-        return found + [2 * chip + 1 - core]
-
-    pairs = [(step, -step) for step in range(chips // 2 - 1, 0, -1)]
-    out_steps = [chips // 2, *sum(pairs, ())]
-    in_steps = [chips // 2, *sum(pairs[-1:] + pairs[:-1], ())]
+    def others(first):
+        place = lax.rem(me - first + n, n)
+        return [lax.rem(first + i + (place <= i).astype(jnp.int32), n) for i in range(n - 1)]
 
     loads = [pltpu.make_async_copy(src, dst, w_sem.at[i]) for i, (src, dst) in enumerate((
         (g1_hbm, g1), (b1_hbm, b1), (wi_hbm, wi), (bi_hbm, bi), (g2_hbm, g2), (b2_hbm, b2),
@@ -50,7 +40,7 @@
 
     barrier = pltpu.get_barrier_semaphore()
 
-    for to in others(in_steps):
+    for to in others(0):
         pl.semaphore_signal(barrier, inc=1, device_id={"seq": to}, device_id_type=MESH)
     pl.semaphore_wait(barrier, n - 1)
 
@@ -58,7 +48,7 @@
         return pl.ds(pl.multiple_of(base * patches + me * rows, rows), rows)
 
     def send_in(j, carry):
-        for to in others(in_steps):
+        for to in others(n // 2):
             pltpu.make_async_remote_copy(
                 src_ref=x_hbm.at[to, j], dst_ref=gath.at[mine(j)], send_sem=in_send.at[0], recv_sem=in_recv.at[j],
                 device_id={"seq": to}, device_id_type=MESH).start()
@@ -123,7 +113,7 @@
         def rows_of(dev):
             return pl.ds(pl.multiple_of(base + dev * rows, rows), rows)
 
-        for to in others(out_steps):
+        for to in others(0):
             pltpu.make_async_remote_copy(
                 src_ref=ybuf.at[rows_of(to)], dst_ref=out_ref.at[me, j], send_sem=out_send.at[0], recv_sem=out_recv.at[0],
                 device_id={"seq": to}, device_id_type=MESH).start()

time: 101 us -> 102 us (level); the launches traced: 101 us -> 101 us
  no operation moved by 1% of the time
where the time goes in v4:
time: 102 us; the launch traced here: 101 us
  Pallas kernels  99.8 us (98%)
  local copies, waits for them, and re-layouts  1.32 us (1%)
    pallas_call x1, Pallas kernels, per_device(): pl.pallas_call(functools.partial(kernel, n, row_tile, col_tile), out_shap...  99.8 us

profile of v4, /device:TPU:21, one launch (start us, length us, event | category | flops | bytes accessed | tf_op | source)
XLA Modules:
  0.0 101.1 jit_solution(6230892954192085930)
XLA Ops:
  0.0 99.8 %gmlp.1 = bf16[16,4,32,512]{3,2,1,0:T(8,128)(2,1)S(1)} custom-call(bf16[16,4,32,512]{3,2,1,0:T(8,128)(2,1)} %bitcast.8, f32[1,512]{1,0:T(1,128)} %bitcast.10, f32[1,512]{1,0:T(1,128)} %bitcast.11, bf16[512,3072]{1,0:T(8,128)(2,1)} %wi_hbm.1, f32[1,3072]{1,0:T(1,128)} %bitcast.9, f32[1536]{0:T(1024)} %g2_hbm.1, f32[1536]{0:T(1024)} %b2_hbm.1, ...), custom_call_target="tpu_custom_call" | custom-call | tf_op jit(solution)/shard_map/gmlp/pallas_call | solution.py:146
  99.8 1.3 %copy.13 = bf16[64,32,512]{2,1,0:T(8,128)(2,1)} copy(bf16[64,32,512]{2,1,0:T(8,128)(2,1)S(1)} %bitcast.7) | data formatting | bytes 4194304

commit v5 on v3

--- a/solution.py
+++ b/solution.py
@@ -21,7 +21,7 @@
 
 def kernel(n, row_tile, col_tile, x_hbm, g1_hbm, b1_hbm, wi_hbm, bi_hbm, g2_hbm, b2_hbm, ws_hbm, bs_hbm, wo_hbm, bo_hbm,
            out_ref, gath, ybuf, hbuf, nbuf, gbuf, g1, b1, wi, bi, g2, b2, ws, wst, bs, bst, wo, bo,
-           w_sem, in_send, in_recv, out_send, out_recv):
+           answered, complete, w_sem, in_send, in_recv, out_send, out_recv):
     me = lax.axis_index("seq")
     per_dev, rows, chans = x_hbm.shape[1], x_hbm.shape[2], x_hbm.shape[3]
     patches = n * rows
@@ -31,16 +31,15 @@
     chips = n // 2
     chip, core = lax.div(me, 2), lax.rem(me, 2)
 
-    def others(steps):
+    def by_distance():
         found = []
-        for step in steps:
+        for step in [chips // 2, *sum(((step, -step) for step in range(chips // 2 - 1, 0, -1)), ())]:
             there = 2 * lax.rem(chip + step + chips, chips)
             found += [there + core, there + 1 - core]
         return found + [2 * chip + 1 - core]
 
-    pairs = [(step, -step) for step in range(chips // 2 - 1, 0, -1)]
-    out_steps = [chips // 2, *sum(pairs, ())]
-    in_steps = [chips // 2, *sum(pairs[-1:] + pairs[:-1], ())]
+    def by_index():
+        return [i + (me <= i).astype(jnp.int32) for i in range(n - 1)]
 
     loads = [pltpu.make_async_copy(src, dst, w_sem.at[i]) for i, (src, dst) in enumerate((
         (g1_hbm, g1), (b1_hbm, b1), (wi_hbm, wi), (bi_hbm, bi), (g2_hbm, g2), (b2_hbm, b2),
@@ -48,23 +47,60 @@
     for load in loads:
         load.start()
 
-    barrier = pltpu.get_barrier_semaphore()
-
-    for to in others(in_steps):
-        pl.semaphore_signal(barrier, inc=1, device_id={"seq": to}, device_id_type=MESH)
-    pl.semaphore_wait(barrier, n - 1)
-
     def mine(base):
         return pl.ds(pl.multiple_of(base * patches + me * rows, rows), rows)
 
-    def send_in(j, carry):
-        for to in others(in_steps):
-            pltpu.make_async_remote_copy(
-                src_ref=x_hbm.at[to, j], dst_ref=gath.at[mine(j)], send_sem=in_send.at[0], recv_sem=in_recv.at[j],
-                device_id={"seq": to}, device_id_type=MESH).start()
+    def send_in(j, to):
+        pltpu.make_async_remote_copy(
+            src_ref=x_hbm.at[to, j], dst_ref=gath.at[mine(j)], send_sem=in_send.at[0], recv_sem=in_recv.at[j],
+            device_id={"seq": to}, device_id_type=MESH).start()
+
+    barrier = pltpu.get_barrier_semaphore()
+    span = n // 2
+    low = me < span
+    early = per_dev // 2
+
+    def tell(sem, to):
+        pl.semaphore_signal(sem, inc=1, device_id={"seq": to}, device_id_type=MESH)
+
+    def send_early(first):
+        for j in range(early):
+            for to in range(first, first + span):
+                @pl.when(me != to)
+                def _():
+                    send_in(j, to)
+
+    @pl.when(low)
+    def _():
+        for to in by_index():
+            tell(barrier, to)
+
+    pl.semaphore_wait(barrier, span - low.astype(jnp.int32))
+
+    @pl.when(jnp.logical_not(low))
+    def _():
+        for to in range(span):
+            tell(answered, to)
+
+    send_early(0)
+
+    @pl.when(low)
+    def _():
+        pl.semaphore_wait(answered, span)
+        tell(complete, n - 1 - me)
+
+    @pl.when(jnp.logical_not(low))
+    def _():
+        pl.semaphore_wait(complete, 1)
+
+    send_early(span)
+
+    def send_late(j, carry):
+        for to in by_distance():
+            send_in(j, to)
         return carry
 
-    lax.fori_loop(0, per_dev, send_in, 0)
+    lax.fori_loop(early, per_dev, send_late, 0)
     for j in range(per_dev):
         pltpu.make_async_copy(x_hbm.at[me, j], gath.at[mine(j)], in_recv.at[j]).start()
 
@@ -123,10 +159,14 @@
         def rows_of(dev):
             return pl.ds(pl.multiple_of(base + dev * rows, rows), rows)
 
-        for to in others(out_steps):
+        def send_out(to):
             pltpu.make_async_remote_copy(
                 src_ref=ybuf.at[rows_of(to)], dst_ref=out_ref.at[me, j], send_sem=out_send.at[0], recv_sem=out_recv.at[0],
                 device_id={"seq": to}, device_id_type=MESH).start()
+
+        last = j == per_dev - 1
+        for far, low in zip(by_distance(), by_index()):
+            send_out(jnp.where(last, low, far))
         pltpu.make_async_copy(ybuf.at[rows_of(me)], out_ref.at[me, j], out_recv.at[0]).start()
         return carry
 
@@ -170,6 +210,7 @@
                 vmem((total, total), bf16), vmem((total, total), bf16),
                 vmem((1, total), f32), vmem((total, 128), f32),
                 vmem((half, chans), bf16), vmem((1, chans), f32),
+                pltpu.SemaphoreType.REGULAR, pltpu.SemaphoreType.REGULAR,
                 dma((10,)), dma((1,)), dma((per_dev,)), dma((1,)), dma((1,)),
             ],
             compiler_params=pltpu.CompilerParams(

time: 101 us -> 99.6 us (0.986); the launches traced: 101 us -> 98.4 us
  Pallas kernels: 100 us -> 97.1 us
    pallas_call x1, Pallas kernels: 100 us -> 97.1 us  [per_device(): pl.pallas_call(functools.partial(kernel, n, row_tile, col_tile), out_shap...]
where the time goes in v5:
time: 99.6 us; the launch traced here: 98.4 us
  Pallas kernels  97.1 us (97%)
  local copies, waits for them, and re-layouts  1.32 us (1%)
    pallas_call x1, Pallas kernels, per_device(): pl.pallas_call(functools.partial(kernel, n, row_tile, col_tile), out_shap...  97.1 us

profile of v5, /device:TPU:21, one launch (start us, length us, event | category | flops | bytes accessed | tf_op | source)
XLA Modules:
  0.0 98.4 jit_solution(9476668235117960791)
XLA Ops:
  0.0 97.1 %gmlp.1 = bf16[16,4,32,512]{3,2,1,0:T(8,128)(2,1)S(1)} custom-call(bf16[16,4,32,512]{3,2,1,0:T(8,128)(2,1)} %bitcast.8, f32[1,512]{1,0:T(1,128)} %bitcast.10, f32[1,512]{1,0:T(1,128)} %bitcast.11, bf16[512,3072]{1,0:T(8,128)(2,1)} %wi_hbm.1, f32[1,3072]{1,0:T(1,128)} %bitcast.9, f32[1536]{0:T(1024)} %g2_hbm.1, f32[1536]{0:T(1024)} %b2_hbm.1, ...), custom_call_target="tpu_custom_call" | custom-call | tf_op jit(solution)/shard_map/gmlp/pallas_call | solution.py:196
  97.1 1.3 %copy.13 = bf16[64,32,512]{2,1,0:T(8,128)(2,1)} copy(bf16[64,32,512]{2,1,0:T(8,128)(2,1)S(1)} %bitcast.7) | data formatting | bytes 4194304

commit v6 on v5

--- a/solution.py
+++ b/solution.py
@@ -10,6 +10,9 @@
 LN_EPS = 1e-6
 MESH = pl.DeviceIdType.MESH
 SQRT_HALF = 0.7071067811865476
+GREET_STEPS = (4, 2, -2, 3, -3, 1, -1, 0)
+IN_STEPS = (-2, 0, -1, 3, 2, 1, 4, -3)
+OUT_STEPS = (4, 3, -3, -1, -2, 1, 0, 2)
 
 
 def normalize(values_f, gain_vec, offset):
@@ -31,12 +34,13 @@
     chips = n // 2
     chip, core = lax.div(me, 2), lax.rem(me, 2)
 
-    def by_distance():
+    def ring(steps):
         found = []
-        for step in [chips // 2, *sum(((step, -step) for step in range(chips // 2 - 1, 0, -1)), ())]:
+        for step in steps:
             there = 2 * lax.rem(chip + step + chips, chips)
-            found += [there + core, there + 1 - core]
-        return found + [2 * chip + 1 - core]
+            found += [there + core, there + 1 - core] if step else [there + 1 - core]
+        assert len(found) == n - 1
+        return found
 
     def by_index():
         return [i + (me <= i).astype(jnp.int32) for i in range(n - 1)]
@@ -44,8 +48,6 @@
     loads = [pltpu.make_async_copy(src, dst, w_sem.at[i]) for i, (src, dst) in enumerate((
         (g1_hbm, g1), (b1_hbm, b1), (wi_hbm, wi), (bi_hbm, bi), (g2_hbm, g2), (b2_hbm, b2),
         (ws_hbm, ws), (bs_hbm, bs), (wo_hbm, wo), (bo_hbm, bo)))]
-    for load in loads:
-        load.start()
 
     def mine(base):
         return pl.ds(pl.multiple_of(base * patches + me * rows, rows), rows)
@@ -58,7 +60,7 @@
     barrier = pltpu.get_barrier_semaphore()
     span = n // 2
     low = me < span
-    early = per_dev // 2
+    early = 2
 
     def tell(sem, to):
         pl.semaphore_signal(sem, inc=1, device_id={"seq": to}, device_id_type=MESH)
@@ -72,9 +74,11 @@
 
     @pl.when(low)
     def _():
-        for to in by_index():
+        for to in ring(GREET_STEPS):
             tell(barrier, to)
 
+    for load in loads:
+        load.start()
     pl.semaphore_wait(barrier, span - low.astype(jnp.int32))
 
     @pl.when(jnp.logical_not(low))
@@ -96,7 +100,7 @@
     send_early(span)
 
     def send_late(j, carry):
-        for to in by_distance():
+        for to in ring(IN_STEPS):
             send_in(j, to)
         return carry
 
@@ -165,7 +169,7 @@
                 device_id={"seq": to}, device_id_type=MESH).start()
 
         last = j == per_dev - 1
-        for far, low in zip(by_distance(), by_index()):
+        for far, low in zip(ring(OUT_STEPS), by_index()):
             send_out(jnp.where(last, low, far))
         pltpu.make_async_copy(ybuf.at[rows_of(me)], out_ref.at[me, j], out_recv.at[0]).start()
         return carry

time: 99.6 us -> 98.6 us (0.990)
  no operation moved by 1% of the time
where the time goes in v6:
time: 98.6 us; the launch traced here: 97.8 us
  Pallas kernels  96.5 us (98%)
  local copies, waits for them, and re-layouts  1.32 us (1%)
    pallas_call x1, Pallas kernels, per_device(): pl.pallas_call(functools.partial(kernel, n, row_tile, col_tile), out_shap...  96.5 us

profile of v6, /device:TPU:21, one launch (start us, length us, event | category | flops | bytes accessed | tf_op | source)
XLA Modules:
  0.0 97.8 jit_solution(14639635714893498253)
XLA Ops:
  0.0 96.5 %gmlp.1 = bf16[16,4,32,512]{3,2,1,0:T(8,128)(2,1)S(1)} custom-call(bf16[16,4,32,512]{3,2,1,0:T(8,128)(2,1)} %bitcast.8, f32[1,512]{1,0:T(1,128)} %bitcast.10, f32[1,512]{1,0:T(1,128)} %bitcast.11, bf16[512,3072]{1,0:T(8,128)(2,1)} %wi_hbm.1, f32[1,3072]{1,0:T(1,128)} %bitcast.9, f32[1536]{0:T(1024)} %g2_hbm.1, f32[1536]{0:T(1024)} %b2_hbm.1, ...), custom_call_target="tpu_custom_call" | custom-call | tf_op jit(solution)/shard_map/gmlp/pallas_call | solution.py:200
  96.5 1.3 %copy.13 = bf16[64,32,512]{2,1,0:T(8,128)(2,1)} copy(bf16[64,32,512]{2,1,0:T(8,128)(2,1)S(1)} %bitcast.7) | data formatting | bytes 4194304

commit v7 on v6

--- a/solution.py
+++ b/solution.py
@@ -83,7 +83,7 @@
 
     @pl.when(jnp.logical_not(low))
     def _():
-        for to in range(span):
+        for to in range(span - 1, -1, -1):
             tell(answered, to)
 
     send_early(0)

time: 98.6 us -> 98.5 us (level)
  no operation moved by 1% of the time
where the time goes in v7:
time: 98.5 us; the launch traced here: 98.3 us
  Pallas kernels  96.9 us (98%)
  local copies, waits for them, and re-layouts  1.32 us (1%)
    pallas_call x1, Pallas kernels, per_device(): pl.pallas_call(functools.partial(kernel, n, row_tile, col_tile), out_shap...  96.9 us

profile of v7, /device:TPU:21, one launch (start us, length us, event | category | flops | bytes accessed | tf_op | source)
XLA Modules:
  0.0 98.3 jit_solution(10324011324392317435)
XLA Ops:
  0.0 96.9 %gmlp.1 = bf16[16,4,32,512]{3,2,1,0:T(8,128)(2,1)S(1)} custom-call(bf16[16,4,32,512]{3,2,1,0:T(8,128)(2,1)} %bitcast.8, f32[1,512]{1,0:T(1,128)} %bitcast.10, f32[1,512]{1,0:T(1,128)} %bitcast.11, bf16[512,3072]{1,0:T(8,128)(2,1)} %wi_hbm.1, f32[1,3072]{1,0:T(1,128)} %bitcast.9, f32[1536]{0:T(1024)} %g2_hbm.1, f32[1536]{0:T(1024)} %b2_hbm.1, ...), custom_call_target="tpu_custom_call" | custom-call | tf_op jit(solution)/shard_map/gmlp/pallas_call | solution.py:200
  96.9 1.3 %copy.13 = bf16[64,32,512]{2,1,0:T(8,128)(2,1)} copy(bf16[64,32,512]{2,1,0:T(8,128)(2,1)S(1)} %bitcast.7) | data formatting | bytes 4194304

commit v8 on v7

--- a/solution.py
+++ b/solution.py
@@ -77,16 +77,16 @@
         for to in ring(GREET_STEPS):
             tell(barrier, to)
 
+    pl.semaphore_wait(barrier, span - low.astype(jnp.int32))
+
+    @pl.when(jnp.logical_not(low))
+    def _():
+        for to in range(span - 1, -1, -1):
+            tell(answered, to)
+
+    send_early(0)
     for load in loads:
         load.start()
-    pl.semaphore_wait(barrier, span - low.astype(jnp.int32))
-
-    @pl.when(jnp.logical_not(low))
-    def _():
-        for to in range(span - 1, -1, -1):
-            tell(answered, to)
-
-    send_early(0)
 
     @pl.when(low)
     def _():

time: 98.5 us -> 98.3 us (level)
  no operation moved by 1% of the time
where the time goes in v8:
time: 98.3 us
  Pallas kernels  96.9 us (99%)
  local copies, waits for them, and re-layouts  1.32 us (1%)
    pallas_call x1, Pallas kernels, per_device(): pl.pallas_call(functools.partial(kernel, n, row_tile, col_tile), out_shap...  96.9 us

profile of v8, /device:TPU:21, one launch (start us, length us, event | category | flops | bytes accessed | tf_op | source)
XLA Modules:
  0.0 98.3 jit_solution(2162665351811105914)
XLA Ops:
  0.0 96.9 %gmlp.1 = bf16[16,4,32,512]{3,2,1,0:T(8,128)(2,1)S(1)} custom-call(bf16[16,4,32,512]{3,2,1,0:T(8,128)(2,1)} %bitcast.8, f32[1,512]{1,0:T(1,128)} %bitcast.10, f32[1,512]{1,0:T(1,128)} %bitcast.11, bf16[512,3072]{1,0:T(8,128)(2,1)} %wi_hbm.1, f32[1,3072]{1,0:T(1,128)} %bitcast.9, f32[1536]{0:T(1024)} %g2_hbm.1, f32[1536]{0:T(1024)} %b2_hbm.1, ...), custom_call_target="tpu_custom_call" | custom-call | tf_op jit(solution)/shard_map/gmlp/pallas_call | solution.py:200
  96.9 1.3 %copy.13 = bf16[64,32,512]{2,1,0:T(8,128)(2,1)} copy(bf16[64,32,512]{2,1,0:T(8,128)(2,1)S(1)} %bitcast.7) | data formatting | bytes 4194304
